TPU v7x, 32 devices: a whole 2x2x4 slice. The times are simulated.
32 devices in a mesh: groups: 2 (over y), rows: 4 (over z), sub: 4 (over x, core).
Axes of the slice: x: 2, y: 2, z: 4, core: 2. Of those that a mesh axis runs over, the one named last changes fastest.
Arguments:
- matrix: float32 [16384, 1024], P(('groups', 'rows', 'sub')), parts along dimension 0
- sign_bits: int32 [16384], P(('groups', 'rows', 'sub')), parts along dimension 0, may hold values from 0 to 1
- samples: int32 [8192], P('groups'), parts along dimension 0, may hold values from 0 to 8191
Outputs:
- cholesky_factor: float32 [2048, 1024], P('groups'), parts along dimension 0
There are 2 independent parts, one for each index of `groups`. A program takes and returns all parts, laid end to end along the dimension named above; each array names one. Nothing has to cross between parts.
Inputs may be any that keep to these rules, and one draw needn't show every extreme that they name: `samples`: row numbers of the whole matrix, drawn independently; a row may be drawn more than once.
All inputs are finite; a program needn't handle non-finite values.
Results may differ from a plain program's by a relative error of at most 0.00011.
Values sent between devices are 32-bit elements; how exact they have to be, the bound alone decides.
A program may use at most 64 MiB of HBM per device.

v0:
```python
import jax
import jax.numpy as jnp
from jax import lax
from jax.sharding import PartitionSpec as P

HIGHEST = lax.Precision.HIGHEST


def hadamard_table(extent):
    line_ids = jnp.arange(extent, dtype=jnp.int32)
    correlation = jnp.bitwise_and(line_ids[:, None], line_ids[None, :])
    parity = jnp.zeros((extent, extent), jnp.int32)
    for bit_pos in range(extent.bit_length() - 1):
        parity = parity + jnp.bitwise_and(jnp.right_shift(correlation, bit_pos), 1)
    return (1 - 2 * (parity % 2)).astype(jnp.float32)


def local_transform(values):
    rows_here, columns = values.shape
    inner_size = min(rows_here, 128)
    outer_size = rows_here // inner_size
    blocks = values.reshape(outer_size, inner_size, columns)
    blocks = jnp.einsum("ab,qbn->qan", hadamard_table(inner_size), blocks, precision=HIGHEST)
    blocks = jnp.einsum("pq,qan->pan", hadamard_table(outer_size), blocks, precision=HIGHEST)
    return blocks.reshape(rows_here, columns)


def mix_sources(received):
    return jnp.einsum("ab,bjn->ajn", hadamard_table(received.shape[0]), received, precision=HIGHEST)


def body(matrix, sign_bits, samples):
    rows_here, columns = matrix.shape
    devices = lax.axis_size(("rows", "sub"))
    position = lax.axis_index(("rows", "sub"))
    per_block = rows_here // devices
    sign_values = (2 * sign_bits - 1).astype(jnp.float32)
    current = local_transform(matrix * sign_values[:, None])
    block_ids = (
        (jnp.arange(devices, dtype=jnp.int32) * rows_here)[:, None]
        + position * per_block
        + jnp.arange(per_block, dtype=jnp.int32)[None, :]
    )
    blocks = current.reshape(devices, per_block, columns)
    mixed_rows = mix_sources(
        lax.all_to_all(blocks, ("rows", "sub"), split_axis=0, concat_axis=0, tiled=True)
    )
    owned_rows = mixed_rows.reshape(rows_here, columns)
    row_ids = block_ids.reshape(rows_here)
    matches = (row_ids[:, None] == samples[None, :]).astype(jnp.float32)
    counts = jnp.sum(matches, axis=1)
    weighted = owned_rows * counts[:, None]
    total_rows = rows_here * devices
    own_terms = jnp.einsum("rn,rm->nm", weighted, owned_rows, precision=HIGHEST) / jnp.float32(
        total_rows * samples.shape[0]
    )
    gram_matrix = lax.psum(own_terms, ("rows", "sub"))
    return jnp.linalg.cholesky(gram_matrix)


def solution(mesh):
    placed = (P(("groups", "rows", "sub"), None), P(("groups", "rows", "sub")), P("groups"))
    return jax.shard_map(
        body, mesh=mesh, in_specs=placed, out_specs=P("groups", None), check_vma=False
    )
```

profile of v0, /device:TPU:0, one launch (start us, length us, event | category | flops | bytes accessed | tf_op | source)
XLA Modules:
  0.0 427.4 jit_solution(5437568680601087725)
XLA Ops:
  9.0 3.5 convolution_bitcast_fusion
  14.5 5.4 %fusion.69 = f32[4,128,1024]{2,0,1:T(4,128)S(1)} fusion(f32[4,128,1024]{2,0,1:T(4,128)} %copy.23), kind=kOutput, calls=%fused_computation.112 | convolution fusion | flops 25166144 | bytes 4194304 | tf_op jit(solution)/shard_map/pq,qan->pan/dot_general | solution.py:24
  19.9 2.5 copy.24
  22.4 7.4 %all-to-all-start = ((f32[16,32,1024]{2,1,0:T(8,128)}), f32[16,32,1024]{2,1,0:T(8,128)S(1)}, u32[]{:S(2)}, u32[]{:S(2)}) async-start(f32[16,32,1024]{2,1,0:T(8,128)} %bitcast.60), calls=%async_computation | async-start | bytes 4194304 | tf_op jit(solution)/shard_map/all_to_all | solution.py:46
  31.7 39.1 %all-to-all-done = f32[16,32,1024]{2,1,0:T(8,128)S(1)} async-done(((f32[16,32,1024]{2,1,0:T(8,128)}), f32[16,32,1024]{2,1,0:T(8,128)S(1)}, u32[]{:S(2)}, u32[]{:S(2)}) %all-to-all-start) | async-done | bytes 2097184 | tf_op jit(solution)/shard_map/all_to_all | solution.py:46
  70.8 2.9 fusion.5
  73.7 8.9 %bitcast_multiply_fusion = f32[1024,1024]{0,1:T(8,128)} fusion(f32[16,32,1024]{2,0,1:T(8,128)S(1)} %fusion.5, f32[16,32]{0,1:T(8,128)S(1)} %copy.26), kind=kOutput, calls=%fused_computation.3 | convolution fusion | flops 6444023808 | bytes 6293504 | tf_op jit(solution)/shard_map/rn,rm->nm/dot_general | solution.py:54
  82.6 118.0 %all-reduce.3.cloned.1.call-done = f32[1024,1024]{0,1:T(8,128)} async-done(((f32[1024,1024]{0,1:T(8,128)}), f32[1024,1024]{0,1:T(8,128)}) %all-reduce.3.cloned.1.call-update) | async-done | bytes 4194320 | tf_op jit(solution)/shard_map/psum | solution.py:57
  200.6 5.5 %copy.28 = f32[1024,1024]{1,0:T(8,128)} copy(f32[1024,1024]{0,1:T(8,128)} %all-reduce.3.cloned.1.call-done) | data formatting | bytes 8388608 | tf_op jit(solution)/shard_map/psum | solution.py:57
  206.1 4.4 %fusion = f32[1024,1024]{1,0:T(8,128)S(1)} fusion(f32[1024,1024]{1,0:T(8,128)} %copy.28, f32[1024,1024]{0,1:T(8,128)} %all-reduce.3.cloned.1.call-done), kind=kLoop, calls=%fused_computation.2 | loop fusion | flops 2097152 | bytes 12582912 | tf_op jit(solution)/shard_map/jit(cholesky)/div | solution.py:58
  212.5 11.7 %cholesky.223 = f32[128,128]{1,0:T(8,128)S(1)} custom-call(f32[128,128]{1,0:T(8,128)S(1)} %cholesky.580), custom_call_target="Cholesky" | custom-call | tf_op jit(solution)/shard_map/jit(cholesky)/cholesky | solution.py:58
  224.2 9.8 %custom-call.59 = f32[1,128,128]{1,2,0:T(8,128)S(1)} custom-call(f32[1,128,128]{2,1,0:T(8,128)S(1)} %get-tuple-element.26), custom_call_target="InvertDiagBlocksLowerTriangular" | custom-call | tf_op jit(solution)/shard_map/jit(cholesky)/cholesky | solution.py:58
  234.0 2.5 cholesky.255
  236.6 2.3 constant_dynamic-update-slice_fusion.5
  240.4 11.9 %cholesky.244 = f32[128,128]{1,0:T(8,128)S(1)} custom-call(f32[128,128]{1,0:T(8,128)S(1)} %cholesky.584), custom_call_target="Cholesky" | custom-call | tf_op jit(solution)/shard_map/jit(cholesky)/cholesky | solution.py:58
  253.0 9.8 %custom-call.60 = f32[1,128,128]{1,2,0:T(8,128)S(1)} custom-call(f32[1,128,128]{2,1,0:T(8,128)S(1)} %get-tuple-element.23), custom_call_target="InvertDiagBlocksLowerTriangular" | custom-call | tf_op jit(solution)/shard_map/jit(cholesky)/cholesky | solution.py:58
  264.0 2.1 convolution_subtract_fusion.1
  266.1 11.7 %cholesky.468 = f32[128,128]{1,0:T(8,128)S(1)} custom-call(f32[128,128]{1,0:T(8,128)S(1)} %cholesky.589), custom_call_target="Cholesky" | custom-call | tf_op jit(solution)/shard_map/jit(cholesky)/cholesky | solution.py:58
  279.1 9.8 %custom-call.61 = f32[1,128,128]{1,2,0:T(8,128)S(1)} custom-call(f32[1,128,128]{2,1,0:T(8,128)S(1)} %get-tuple-element.20), custom_call_target="InvertDiagBlocksLowerTriangular" | custom-call | tf_op jit(solution)/shard_map/jit(cholesky)/cholesky | solution.py:58
  290.1 2.3 convolution_subtract_fusion.2
  292.4 12.1 %cholesky.487 = f32[128,128]{1,0:T(8,128)S(1)} custom-call(f32[128,128]{1,0:T(8,128)S(1)} %cholesky.594), custom_call_target="Cholesky" | custom-call | tf_op jit(solution)/shard_map/jit(cholesky)/cholesky | solution.py:58
  305.8 9.8 %custom-call.62 = f32[1,128,128]{1,2,0:T(8,128)S(1)} custom-call(f32[1,128,128]{2,1,0:T(8,128)S(1)} %get-tuple-element.17), custom_call_target="InvertDiagBlocksLowerTriangular" | custom-call | tf_op jit(solution)/shard_map/jit(cholesky)/cholesky | solution.py:58
  316.7 2.3 convolution_subtract_fusion.3
  319.1 11.7 %cholesky.506 = f32[128,128]{1,0:T(8,128)S(1)} custom-call(f32[128,128]{1,0:T(8,128)S(1)} %cholesky.599), custom_call_target="Cholesky" | custom-call | tf_op jit(solution)/shard_map/jit(cholesky)/cholesky | solution.py:58
  332.1 10.0 %custom-call.63 = f32[1,128,128]{1,2,0:T(8,128)S(1)} custom-call(f32[1,128,128]{2,1,0:T(8,128)S(1)} %get-tuple-element.14), custom_call_target="InvertDiagBlocksLowerTriangular" | custom-call | tf_op jit(solution)/shard_map/jit(cholesky)/cholesky | solution.py:58
  343.1 2.3 convolution_subtract_fusion.4
  345.4 11.7 %cholesky.526 = f32[128,128]{1,0:T(8,128)S(1)} custom-call(f32[128,128]{1,0:T(8,128)S(1)} %cholesky.604), custom_call_target="Cholesky" | custom-call | tf_op jit(solution)/shard_map/jit(cholesky)/cholesky | solution.py:58
  358.4 9.8 %custom-call.64 = f32[1,128,128]{1,2,0:T(8,128)S(1)} custom-call(f32[1,128,128]{2,1,0:T(8,128)S(1)} %get-tuple-element.11), custom_call_target="InvertDiagBlocksLowerTriangular" | custom-call | tf_op jit(solution)/shard_map/jit(cholesky)/cholesky | solution.py:58
  371.2 11.9 %cholesky.546 = f32[128,128]{1,0:T(8,128)S(1)} custom-call(f32[128,128]{1,0:T(8,128)S(1)} %cholesky.609), custom_call_target="Cholesky" | custom-call | tf_op jit(solution)/shard_map/jit(cholesky)/cholesky | solution.py:58
  384.4 9.8 %custom-call.65 = f32[1,128,128]{1,2,0:T(8,128)S(1)} custom-call(f32[1,128,128]{2,1,0:T(8,128)S(1)} %get-tuple-element.8), custom_call_target="InvertDiagBlocksLowerTriangular" | custom-call | tf_op jit(solution)/shard_map/jit(cholesky)/cholesky | solution.py:58
  396.8 11.7 %cholesky.564 = f32[128,128]{1,0:T(8,128)S(1)} custom-call(f32[128,128]{1,0:T(8,128)S(1)} %convolution_subtract_fusion.6), custom_call_target="Cholesky" | custom-call | tf_op jit(solution)/shard_map/jit(cholesky)/cholesky | solution.py:58
  415.5 4.9 %select_select_fusion = f32[1024,1024]{1,0:T(8,128)} fusion(f32[1024,1024]{1,0:T(8,128)} %get-tuple-element.6, pred[]{:T(512)S(6)} %cholesky.579), kind=kLoop, calls=%fused_computation.4 | loop fusion | flops 3145728 | bytes 8388609 | tf_op jit(solution)/shard_map/jit(cholesky)/select_n | solution.py:58
  (46 shorter events, 29.1 us)
Async XLA Ops:
  19.9 10.6 %copy-start.1 = (s32[4096]{0:T(1024)S(1)}, s32[4096]{0:T(1024)}, u32[]{:S(2)}) copy-start(s32[4096]{0:T(1024)} %param.5) | copy-start | bytes 49156
  22.4 48.4 %all-to-all-start = ((f32[16,32,1024]{2,1,0:T(8,128)}), f32[16,32,1024]{2,1,0:T(8,128)S(1)}, u32[]{:S(2)}, u32[]{:S(2)}) async-start(f32[16,32,1024]{2,1,0:T(8,128)} %bitcast.60), calls=%async_computation | async-start | bytes 4194304 | tf_op jit(solution)/shard_map/all_to_all | solution.py:46
  29.8 170.8 %all-reduce.3.cloned.1.call-start = ((), (), s32[]{:S(2)}) async-start(), calls=%async_computation.1 | async-start | bytes 8388608 | tf_op jit(solution)/shard_map/psum | solution.py:57
  210.5 1.9 copy-start
Sparse Core Ops, SparseCore 0:
  82.7 117.8 all-reduce.2
where the time goes:
time: 435 us; the launch traced here: 427 us
  other arithmetic  185 us (43%)
  waiting for transfers between devices  157 us (36%)
  matrix products  43.5 us (10%)
  between operations  18.8 us (4%)
  local copies, waits for them, and re-layouts  14.7 us (3%)
  starting transfers between devices  7.89 us (2%)
    another operation x30, other arithmetic, body(): return jnp.linalg.cholesky(gram_matrix)  172 us
    psum x1, waiting for transfers between devices, body(): gram_matrix = lax.psum(own_terms, ('rows', 'sub'))  118 us
    all_to_all x1, waiting for transfers between devices, body(): lax.all_to_all(blocks, ('rows', 'sub'), split_axis=0, concat_axis=0, tile...  39.1 us
    another operation x14, matrix products, body(): return jnp.linalg.cholesky(gram_matrix)  22.9 us
    dot_general x1, matrix products, body(): jnp.einsum('rn,rm->nm', weighted, owned_rows, precision=HIGHEST)  8.89 us
  transfers between devices with their start and end apart: 2, of which 2 were waited for; matrix products, arithmetic and copies ran while one was open for 0% of the time, Pallas kernels for 0%

commit v1 on v0

--- a/solution.py
+++ b/solution.py
@@ -54,7 +54,7 @@
     own_terms = jnp.einsum("rn,rm->nm", weighted, owned_rows, precision=HIGHEST) / jnp.float32(
         total_rows * samples.shape[0]
     )
-    gram_matrix = lax.psum(own_terms, ("rows", "sub"))
+    gram_matrix = lax.psum(lax.psum(own_terms, "sub"), "rows")
     return jnp.linalg.cholesky(gram_matrix)
 
 

time: 435 us -> 567 us (1.30)
  waiting for transfers between devices: 157 us -> 289 us
    psum x1 -> x2, waiting for transfers between devices: 118 us -> 250 us  [body(): gram_matrix = lax.psum(lax.psum(own_terms, 'sub'), 'rows')]
  transfers between devices with their start and end apart: 2 -> 3, of which waited for: 2 -> 3; matrix products, arithmetic and copies ran while one was open for 0% -> 0% of each run, Pallas kernels for 0% -> 0%
where the time goes in v1:
time: 567 us; the launch traced here: 559 us
  waiting for transfers between devices  289 us (51%)
  other arithmetic  185 us (33%)
  matrix products  43.5 us (8%)
  between operations  18.8 us (3%)
  local copies, waits for them, and re-layouts  14.7 us (3%)
  starting transfers between devices  7.93 us (1%)
    psum x2, waiting for transfers between devices, body(): gram_matrix = lax.psum(lax.psum(own_terms, 'sub'), 'rows')  250 us
    another operation x30, other arithmetic, body(): return jnp.linalg.cholesky(gram_matrix)  172 us
    all_to_all x1, waiting for transfers between devices, body(): lax.all_to_all(blocks, ('rows', 'sub'), split_axis=0, concat_axis=0, tile...  39.1 us
    another operation x14, matrix products, body(): return jnp.linalg.cholesky(gram_matrix)  22.9 us
  transfers between devices with their start and end apart: 3, of which 3 were waited for; matrix products, arithmetic and copies ran while one was open for 0% of the time, Pallas kernels for 0%

profile of v1, /device:TPU:0, one launch (start us, length us, event | category | flops | bytes accessed | tf_op | source)
XLA Modules:
  0.0 559.1 jit_solution(2820878943944639255)
XLA Ops:
  9.0 3.5 convolution_bitcast_fusion
  14.5 5.4 fusion.69
  19.9 2.5 copy.24
  22.4 7.4 %all-to-all-start = ((f32[16,32,1024]{2,1,0:T(8,128)}), f32[16,32,1024]{2,1,0:T(8,128)S(1)}, u32[]{:S(2)}, u32[]{:S(2)}) async-start(f32[16,32,1024]{2,1,0:T(8,128)} %bitcast.60), calls=%async_computation | async-start | bytes 4194304 | tf_op jit(solution)/shard_map/all_to_all | solution.py:46
  31.7 39.1 %all-to-all-done = f32[16,32,1024]{2,1,0:T(8,128)S(1)} async-done(((f32[16,32,1024]{2,1,0:T(8,128)}), f32[16,32,1024]{2,1,0:T(8,128)S(1)}, u32[]{:S(2)}, u32[]{:S(2)}) %all-to-all-start) | async-done | bytes 2097184 | tf_op jit(solution)/shard_map/all_to_all | solution.py:46
  70.8 2.9 fusion.5
  73.7 8.9 %bitcast_multiply_fusion = f32[1024,1024]{0,1:T(8,128)} fusion(f32[16,32,1024]{2,0,1:T(8,128)S(1)} %fusion.5, f32[16,32]{0,1:T(8,128)S(1)} %copy.26), kind=kOutput, calls=%fused_computation.3 | convolution fusion | flops 6444023808 | bytes 6293504 | tf_op jit(solution)/shard_map/rn,rm->nm/dot_general | solution.py:54
  82.6 92.2 %all-reduce.4.cloned.1.call-done = f32[1024,1024]{0,1:T(8,128)} async-done(((f32[1024,1024]{0,1:T(8,128)}), f32[1024,1024]{0,1:T(8,128)}) %all-reduce.4.cloned.1.call-update) | async-done | bytes 4194320 | tf_op jit(solution)/shard_map/psum | solution.py:57
  174.8 157.5 %all-reduce.6.cloned.1.call-done = f32[1024,1024]{0,1:T(8,128)} async-done(((f32[1024,1024]{0,1:T(8,128)}), f32[1024,1024]{0,1:T(8,128)}) %all-reduce.6.cloned.1.call-update) | async-done | bytes 4194320 | tf_op jit(solution)/shard_map/psum | solution.py:57
  332.3 5.5 copy.28
  337.8 4.4 fusion
  344.2 11.7 %cholesky.223 = f32[128,128]{1,0:T(8,128)S(1)} custom-call(f32[128,128]{1,0:T(8,128)S(1)} %cholesky.580), custom_call_target="Cholesky" | custom-call | tf_op jit(solution)/shard_map/jit(cholesky)/cholesky | solution.py:58
  356.0 9.8 %custom-call.59 = f32[1,128,128]{1,2,0:T(8,128)S(1)} custom-call(f32[1,128,128]{2,1,0:T(8,128)S(1)} %get-tuple-element.26), custom_call_target="InvertDiagBlocksLowerTriangular" | custom-call | tf_op jit(solution)/shard_map/jit(cholesky)/cholesky | solution.py:58
  365.8 2.5 cholesky.255
  368.3 2.3 constant_dynamic-update-slice_fusion.5
  372.2 11.9 %cholesky.244 = f32[128,128]{1,0:T(8,128)S(1)} custom-call(f32[128,128]{1,0:T(8,128)S(1)} %cholesky.584), custom_call_target="Cholesky" | custom-call | tf_op jit(solution)/shard_map/jit(cholesky)/cholesky | solution.py:58
  384.7 9.8 %custom-call.60 = f32[1,128,128]{1,2,0:T(8,128)S(1)} custom-call(f32[1,128,128]{2,1,0:T(8,128)S(1)} %get-tuple-element.23), custom_call_target="InvertDiagBlocksLowerTriangular" | custom-call | tf_op jit(solution)/shard_map/jit(cholesky)/cholesky | solution.py:58
  397.9 11.7 %cholesky.468 = f32[128,128]{1,0:T(8,128)S(1)} custom-call(f32[128,128]{1,0:T(8,128)S(1)} %cholesky.589), custom_call_target="Cholesky" | custom-call | tf_op jit(solution)/shard_map/jit(cholesky)/cholesky | solution.py:58
  410.9 9.8 %custom-call.61 = f32[1,128,128]{1,2,0:T(8,128)S(1)} custom-call(f32[1,128,128]{2,1,0:T(8,128)S(1)} %get-tuple-element.20), custom_call_target="InvertDiagBlocksLowerTriangular" | custom-call | tf_op jit(solution)/shard_map/jit(cholesky)/cholesky | solution.py:58
  421.8 2.3 convolution_subtract_fusion.2
  424.2 12.1 %cholesky.487 = f32[128,128]{1,0:T(8,128)S(1)} custom-call(f32[128,128]{1,0:T(8,128)S(1)} %cholesky.594), custom_call_target="Cholesky" | custom-call | tf_op jit(solution)/shard_map/jit(cholesky)/cholesky | solution.py:58
  437.6 9.8 %custom-call.62 = f32[1,128,128]{1,2,0:T(8,128)S(1)} custom-call(f32[1,128,128]{2,1,0:T(8,128)S(1)} %get-tuple-element.17), custom_call_target="InvertDiagBlocksLowerTriangular" | custom-call | tf_op jit(solution)/shard_map/jit(cholesky)/cholesky | solution.py:58
  448.5 2.4 convolution_subtract_fusion.3
  450.8 11.7 %cholesky.506 = f32[128,128]{1,0:T(8,128)S(1)} custom-call(f32[128,128]{1,0:T(8,128)S(1)} %cholesky.599), custom_call_target="Cholesky" | custom-call | tf_op jit(solution)/shard_map/jit(cholesky)/cholesky | solution.py:58
  463.9 10.0 %custom-call.63 = f32[1,128,128]{1,2,0:T(8,128)S(1)} custom-call(f32[1,128,128]{2,1,0:T(8,128)S(1)} %get-tuple-element.14), custom_call_target="InvertDiagBlocksLowerTriangular" | custom-call | tf_op jit(solution)/shard_map/jit(cholesky)/cholesky | solution.py:58
  474.9 2.3 convolution_subtract_fusion.4
  477.2 11.7 %cholesky.526 = f32[128,128]{1,0:T(8,128)S(1)} custom-call(f32[128,128]{1,0:T(8,128)S(1)} %cholesky.604), custom_call_target="Cholesky" | custom-call | tf_op jit(solution)/shard_map/jit(cholesky)/cholesky | solution.py:58
  490.2 9.8 %custom-call.64 = f32[1,128,128]{1,2,0:T(8,128)S(1)} custom-call(f32[1,128,128]{2,1,0:T(8,128)S(1)} %get-tuple-element.11), custom_call_target="InvertDiagBlocksLowerTriangular" | custom-call | tf_op jit(solution)/shard_map/jit(cholesky)/cholesky | solution.py:58
  502.9 11.9 %cholesky.546 = f32[128,128]{1,0:T(8,128)S(1)} custom-call(f32[128,128]{1,0:T(8,128)S(1)} %cholesky.609), custom_call_target="Cholesky" | custom-call | tf_op jit(solution)/shard_map/jit(cholesky)/cholesky | solution.py:58
  516.1 9.8 %custom-call.65 = f32[1,128,128]{1,2,0:T(8,128)S(1)} custom-call(f32[1,128,128]{2,1,0:T(8,128)S(1)} %get-tuple-element.8), custom_call_target="InvertDiagBlocksLowerTriangular" | custom-call | tf_op jit(solution)/shard_map/jit(cholesky)/cholesky | solution.py:58
  528.6 11.7 %cholesky.564 = f32[128,128]{1,0:T(8,128)S(1)} custom-call(f32[128,128]{1,0:T(8,128)S(1)} %convolution_subtract_fusion.6), custom_call_target="Cholesky" | custom-call | tf_op jit(solution)/shard_map/jit(cholesky)/cholesky | solution.py:58
  547.2 4.9 select_select_fusion
  (49 shorter events, 31.2 us)
Async XLA Ops:
  19.9 10.6 %copy-start.1 = (s32[4096]{0:T(1024)S(1)}, s32[4096]{0:T(1024)}, u32[]{:S(2)}) copy-start(s32[4096]{0:T(1024)} %param.5) | copy-start | bytes 49156
  22.4 48.4 %all-to-all-start = ((f32[16,32,1024]{2,1,0:T(8,128)}), f32[16,32,1024]{2,1,0:T(8,128)S(1)}, u32[]{:S(2)}, u32[]{:S(2)}) async-start(f32[16,32,1024]{2,1,0:T(8,128)} %bitcast.60), calls=%async_computation | async-start | bytes 4194304 | tf_op jit(solution)/shard_map/all_to_all | solution.py:46
  29.8 145.0 %all-reduce.4.cloned.1.call-start = ((), (), s32[]{:S(2)}) async-start(), calls=%async_computation.1 | async-start | bytes 8388608 | tf_op jit(solution)/shard_map/psum | solution.py:57
  82.6 249.8 %all-reduce.6.cloned.1.call-start = ((), (), s32[]{:S(2)}) async-start(), calls=%async_computation.2 | async-start | bytes 8388608 | tf_op jit(solution)/shard_map/psum | solution.py:57
  342.3 1.9 copy-start
Sparse Core Ops, SparseCore 0:
  82.7 92.0 all-reduce.3
  177.2 155.1 all-reduce.5
